TPU v7x, 1024 devices: a whole 8x8x8 slice. The times are simulated.
1024 devices in a mesh: seq: 128 (over y_hi, z, x), tp: 8 (over y_lo, core).
Axes of the slice: x: 8, y: 8 (y_hi: 2, y_lo: 4; y = y_hi * 4 + y_lo), z: 8, core: 2. Of those that a mesh axis runs over, the one named last changes fastest.
Arguments:
- query_rows: bfloat16 [24576, 4096], P('seq', 'tp'), may hold values from -120 to 120
- key_rows: bfloat16 [24576, 1024], P('seq', 'tp'), may hold values from -6 to 6
- value_rows: bfloat16 [24576, 1024], P('seq', 'tp'), may hold values from -6 to 6
- document_ids: int32 [24576], replicated, may hold values from 0 to 20, never falling along the last dimension, each value on 1 to 2304 neighbouring positions
- output_weight: bfloat16 [4096, 8192], P('tp'), may hold values from -0.09375 to 0.09375
Outputs:
- attended: bfloat16 [24576, 8192], P(('seq', 'tp'))
Inputs may be any that keep to these rules, and one draw needn't show every extreme that they name: `document_ids`: never falling along the sequence; every document holds at most 2304 tokens, and one holds exactly 2304.
All inputs are finite; a program needn't handle non-finite values.
Results may differ from a plain program's by a relative error of at most 0.014.
Values may be sent and summed in bfloat16 or wider, within the bound.
A program may use at most 32 MiB of HBM per device.

v0:
```python
import jax
import jax.numpy as jnp
from jax import lax
from jax.sharding import PartitionSpec as P

HEADS = 32
KV = 8
HD = 128


def shifted(block, axis, distance):
    devices = range(lax.axis_size(axis))
    route = [(i - distance, i) for i in devices if i - distance in devices]
    return lax.ppermute(block, axis, route)


def per_device(query_rows, key_rows, value_rows, document_ids, output_weight):
    tokens = query_rows.shape[0]
    kv_local = key_rows.shape[1] // HD
    group = HEADS // KV
    seq_total = document_ids.shape[0]
    scaling = 1.0 / HD**0.5
    reach = min(12, lax.axis_size("seq") // 2)
    first_row = lax.axis_index("seq") * tokens
    last_query = first_row + tokens - 1
    queries = query_rows.reshape(tokens, kv_local, group, HD)
    query_doc = lax.dynamic_slice_in_dim(document_ids, first_row, tokens, 0)
    query_pos = first_row + jnp.arange(tokens, dtype=jnp.int32)

    def attend_block(state_in, key_block, value_block, offset):
        key_count = key_block.shape[0]
        padded_doc = jnp.concatenate([jnp.full((key_count,), -1, jnp.int32), document_ids], axis=0)
        doc_start = jnp.clip(offset + key_count, 0, seq_total)
        key_doc = lax.dynamic_slice_in_dim(padded_doc, doc_start, key_count, 0)
        key_pos = offset + jnp.arange(key_count, dtype=jnp.int32)
        allowed = (
            (key_doc[None, :] == query_doc[:, None])
            & (key_pos[None, :] <= query_pos[:, None])
            & (key_pos[None, :] >= 0)
        )

        def update(current):
            running_max, running_sum, accumulated = current
            scores = (
                jnp.einsum(
                    "tkgd,ukd->kgtu",
                    queries,
                    key_block.reshape(key_count, kv_local, HD),
                    preferred_element_type=jnp.float32,
                )
                * scaling
            )
            scores = jnp.where(allowed, scores, -jnp.inf)
            new_max = jnp.maximum(running_max, jnp.max(scores, axis=-1))
            exponent = jnp.exp(scores - new_max[..., None])
            rescale = jnp.exp(running_max - new_max)
            new_sum = running_sum * rescale + jnp.sum(exponent, axis=-1)
            added = jnp.einsum(
                "kgtu,ukd->kgtd",
                exponent.astype(jnp.bfloat16),
                value_block.reshape(key_count, kv_local, HD),
                preferred_element_type=jnp.float32,
            )
            return (new_max, new_sum, accumulated * rescale[..., None] + added)

        block_end = offset + key_count - 1
        probe = jnp.clip(jnp.minimum(block_end, last_query), 0, seq_total - 1)
        probe_doc = lax.dynamic_slice_in_dim(document_ids, probe, 1, 0)[0]
        is_live = (offset <= last_query) & (block_end >= 0) & (probe_doc >= query_doc[0])
        return lax.cond(is_live, update, lambda unchanged: unchanged, state_in)

    initial = (
        jnp.full((kv_local, group, tokens), -1e30, jnp.float32),
        jnp.zeros((kv_local, group, tokens), jnp.float32),
        jnp.zeros((kv_local, group, tokens, HD), jnp.float32),
    )
    collected_keys, collected_values = (key_rows, value_rows)
    count = 1
    while count < reach + 1:
        earlier_keys, earlier_values = shifted((collected_keys, collected_values), "seq", count)
        collected_keys = jnp.concatenate([earlier_keys, collected_keys], axis=0)
        collected_values = jnp.concatenate([earlier_values, collected_values], axis=0)
        count = count * 2
    offset = first_row - (count - 1) * tokens
    key_part = collected_keys
    value_part = collected_values
    part_rows = key_part.shape[0]
    shard_count = part_rows // tokens
    multiple = 1
    while multiple * 2 <= max(1, 1024 // tokens) and shard_count % (multiple * 2) == 0:
        multiple = multiple * 2
    block_rows = multiple * tokens

    def one_block(block_index, current):
        inner = (block_index * block_rows).astype(jnp.int32)
        key_block = lax.dynamic_slice_in_dim(key_part, inner, block_rows, 0)
        value_block = lax.dynamic_slice_in_dim(value_part, inner, block_rows, 0)
        return attend_block(current, key_block, value_block, offset + inner)

    final_state = lax.fori_loop(0, part_rows // block_rows, one_block, initial)
    running_max, running_sum, accumulated = final_state
    context = accumulated / running_sum[..., None]
    context = (
        context.transpose(2, 0, 1, 3).reshape(tokens, kv_local * group * HD).astype(jnp.bfloat16)
    )
    return lax.psum_scatter(
        jnp.dot(context, output_weight, preferred_element_type=jnp.float32).astype(jnp.bfloat16),
        "tp",
        scatter_dimension=0,
        tiled=True,
    )


def solution(mesh):
    in_specs = (P("seq", "tp"), P("seq", "tp"), P("seq", "tp"), P(), P("tp", None))
    out_specs = P(("seq", "tp"), None)
    return jax.shard_map(
        per_device, mesh=mesh, in_specs=in_specs, out_specs=out_specs, check_vma=False
    )
```

profile of v0, /device:TPU:1, one launch (start us, length us, event | category | flops | bytes accessed | tf_op | source)
XLA Modules:
  0.0 183.5 jit_solution(12580981453410973107)
XLA Ops:
  6.5 0.0 copy-start.2
  6.5 0.0 copy-start
  6.5 0.0 reduce-scatter.2.cloned.1.call-start
  6.5 4.1 %collective-permute-start = (bf16[192,128]{1,0:T(8,128)(2,1)}, bf16[192,128]{1,0:T(8,128)(2,1)S(1)}, u32[]{:S(2)}, u32[]{:S(2)}) collective-permute-start(bf16[192,128]{1,0:T(8,128)(2,1)} %param.10), channel_id=1, source_target_pairs={{0,8},{8,16},{16,24},{24,32},{32,40},{40,48},{48,56},{56,64},{64,7... | collective-permute-start | bytes 147464 | tf_op jit(solution)/shard_map/ppermute | solution.py:14
  10.6 3.1 %collective-permute-start.4 = (bf16[192,128]{1,0:T(8,128)(2,1)}, bf16[192,128]{1,0:T(8,128)(2,1)S(1)}, u32[]{:S(2)}, u32[]{:S(2)}) collective-permute-start(bf16[192,128]{1,0:T(8,128)(2,1)} %param.11), channel_id=1, source_target_pairs={{0,8},{8,16},{16,24},{24,32},{32,40},{40,48},{48,56},{56,64},{64,7... | collective-permute-start | bytes 147464 | tf_op jit(solution)/shard_map/ppermute | solution.py:14
  13.7 0.0 collective-permute-done
  13.7 0.8 pad_maximum_fusion.4
  14.6 5.2 %collective-permute-start.1 = (bf16[384,128]{1,0:T(8,128)(2,1)S(1)}, bf16[384,128]{1,0:T(8,128)(2,1)S(1)}, u32[]{:S(2)}, u32[]{:S(2)}) collective-permute-start(bf16[384,128]{1,0:T(8,128)(2,1)S(1)} %pad_maximum_fusion.4), channel_id=1, source_target_pairs={{0,16},{8,24},{16,32},{24,40},{32,48},{40,56},{48,64},{56,72},{64,... | collective-permute-start | bytes 294920 | tf_op jit(solution)/shard_map/ppermute | solution.py:14
  19.8 0.0 collective-permute-done.4
  19.8 0.8 pad_maximum_fusion.5
  20.6 0.0 copy-start.1
  20.6 4.2 %collective-permute-start.5 = (bf16[384,128]{1,0:T(8,128)(2,1)S(1)}, bf16[384,128]{1,0:T(8,128)(2,1)S(1)}, u32[]{:S(2)}, u32[]{:S(2)}) collective-permute-start(bf16[384,128]{1,0:T(8,128)(2,1)S(1)} %pad_maximum_fusion.5), channel_id=1, source_target_pairs={{0,16},{8,24},{16,32},{24,40},{32,48},{40,56},{48,64},{56,72},{64,... | collective-permute-start | bytes 294920 | tf_op jit(solution)/shard_map/ppermute | solution.py:14
  24.8 0.0 collective-permute-done.1
  24.8 0.8 pad_maximum_fusion.2
  25.7 5.7 %collective-permute-start.2 = (bf16[768,128]{1,0:T(8,128)(2,1)S(1)}, bf16[768,128]{1,0:T(8,128)(2,1)S(1)}, u32[]{:S(2)}, u32[]{:S(2)}) collective-permute-start(bf16[768,128]{1,0:T(8,128)(2,1)S(1)} %pad_maximum_fusion.2), channel_id=1, source_target_pairs={{0,32},{8,40},{16,48},{24,56},{32,64},{40,72},{48,80},{56,88},{64,... | collective-permute-start | bytes 589832 | tf_op jit(solution)/shard_map/ppermute | solution.py:14
  31.3 0.0 collective-permute-done.5
  31.4 0.8 pad_maximum_fusion.3
  32.2 6.2 %collective-permute-start.6 = (bf16[768,128]{1,0:T(8,128)(2,1)S(1)}, bf16[768,128]{1,0:T(8,128)(2,1)S(1)}, u32[]{:S(2)}, u32[]{:S(2)}) collective-permute-start(bf16[768,128]{1,0:T(8,128)(2,1)S(1)} %pad_maximum_fusion.3), channel_id=1, source_target_pairs={{0,32},{8,40},{16,48},{24,56},{32,64},{40,72},{48,80},{56,88},{64,... | collective-permute-start | bytes 589832 | tf_op jit(solution)/shard_map/ppermute | solution.py:14
  38.4 0.0 collective-permute-done.2
  38.4 0.8 pad_maximum_fusion
  39.2 4.9 %collective-permute-start.3 = (bf16[1536,128]{1,0:T(8,128)(2,1)S(1)}, bf16[1536,128]{1,0:T(8,128)(2,1)S(1)}, u32[]{:S(2)}, u32[]{:S(2)}) collective-permute-start(bf16[1536,128]{1,0:T(8,128)(2,1)S(1)} %pad_maximum_fusion), channel_id=1, source_target_pairs={{0,64},{8,72},{16,80},{24,88},{32,96},{40,104},{48,112},{56,120},{... | collective-permute-start | bytes 1179656 | tf_op jit(solution)/shard_map/ppermute | solution.py:14
  44.2 1.0 reshape.65
  45.2 0.0 copy-done
  45.2 0.1 dynamic_slice.56
  45.3 0.0 collective-permute-done.6
  45.3 0.0 copy-done.2
  45.3 10.8 %collective-permute-start.7 = (bf16[1536,128]{1,0:T(8,128)(2,1)S(1)}, bf16[1536,128]{1,0:T(8,128)(2,1)S(1)}, u32[]{:S(2)}, u32[]{:S(2)}) collective-permute-start(bf16[1536,128]{1,0:T(8,128)(2,1)S(1)} %pad_maximum_fusion.1), channel_id=1, source_target_pairs={{0,64},{8,72},{16,80},{24,88},{32,96},{40,104},{48,112},{56,120},{... | collective-permute-start | bytes 1179656 | tf_op jit(solution)/shard_map/ppermute | solution.py:14
  56.1 0.0 collective-permute-done.3
  56.2 0.0 copy-done.1
  56.3 7.1 %collective-permute-done.7 = bf16[1536,128]{1,0:T(8,128)(2,1)S(1)} collective-permute-done((bf16[1536,128]{1,0:T(8,128)(2,1)S(1)}, bf16[1536,128]{1,0:T(8,128)(2,1)S(1)}, u32[]{:S(2)}, u32[]{:S(2)}) %collective-permute-start.7) | collective-permute-done | bytes 393248 | tf_op jit(solution)/shard_map/ppermute | solution.py:14
  63.6 12.8 %while.22 = (s32[]{:T(128)}, f32[1,4,192]{2,1,0:T(4,128)S(1)}, f32[1,4,192]{2,1,0:T(4,128)S(1)}, f32[1,4,192,128]{3,2,1,0:T(8,128)S(1)}, s32[]{:T(128)}, /*index...) while((s32[]{:T(128)}, f32[1,4,192]{2,1,0:T(4,128)S(1)}, ...), condition=%wide.region_5.6_spmd.clone, body=%wide.region_0.5_spmd.clone.sunk | while | flops 309269184 | bytes 9220893 | solution.py:100
  63.6 0.6 dynamic_slice.70
  64.2 0.6 slice.15
  66.1 0.6 dynamic_slice.70
  66.8 0.6 slice.15
  68.7 0.6 dynamic_slice.70
  69.3 0.6 slice.15
  71.2 0.6 dynamic_slice.70
  71.8 0.6 slice.15
  73.7 2.7 %conditional.3 = ((f32[1,4,192]{2,1,0:T(4,128)S(1)}, f32[1,4,192]{2,1,0:T(4,128)S(1)}, f32[1,4,192,128]{3,2,1,0:T(8,128)S(1)})) conditional(s32[]{:T(128)} %convert_element_type.45, (f32[1,4,192]{2,1,0:T(4,128)S(1)}, f32[1,4,192]{2,1,0:T(4,128)S(1)}, f32[1,4,192,128]{3,2,1,0:T(8,128)S(1)}) %tuple.78, (s32[24576]{0:T(1024)S(1)}, s32[]{:T(128)}, ...), branch_computations={%region_1.1_spmd, %region_2.4_spmd} | conditional | flops 309269184 | bytes 9216638 | solution.py:70
  73.8 0.1 pad_dynamic-slice_fusion
  73.9 0.2 and_and_fusion
  74.1 0.7 fusion.4
  74.8 0.9 fusion.5
  75.7 0.7 fusion.3
  76.4 0.2 fusion.25
  76.6 0.2 copy.7
  76.8 6.9 %convolution_convert_fusion = bf16[192,8192]{1,0:T(8,128)(2,1)} fusion(bf16[512,8192]{1,0:T(8,128)(2,1)} %param.13, bf16[24,8,4,128]{3,2,1,0:T(4,128)(2,1)S(1)} %bitcast.56), kind=kOutput, calls=%fused_computation.32 | convolution fusion | flops 1612185600 | bytes 11730944 | tf_op jit(solution)/shard_map/dot_general | solution.py:107
  83.6 0.0 reduce-scatter.2.cloned.1.call-update
  83.6 93.1 %reduce-scatter.2.cloned.1.call-done = bf16[24,8192]{1,0:T(8,128)(2,1)} async-done(((bf16[192,8192]{1,0:T(8,128)(2,1)}), bf16[24,8192]{1,0:T(8,128)(2,1)}) %reduce-scatter.2.cloned.1.call-update) | async-done | bytes 393232 | tf_op jit(solution)/shard_map/reduce_scatter | solution.py:106
  (32 shorter events, 0.4 us)
Async XLA Ops:
  6.5 38.8 %copy-start.2 = (bf16[192,128]{1,0:T(8,128)(2,1)S(1)}, bf16[192,128]{1,0:T(8,128)(2,1)}, u32[]{:S(2)}) copy-start(bf16[192,128]{1,0:T(8,128)(2,1)} %param.11) | copy-start | bytes 147460
  6.5 38.7 %copy-start = (s32[24576]{0:T(1024)S(1)}, s32[24576]{0:T(1024)}, u32[]{:S(2)}) copy-start(s32[24576]{0:T(1024)} %param.12) | copy-start | bytes 294916
  6.5 170.2 %reduce-scatter.2.cloned.1.call-start = ((), (), s32[]{:S(2)}) async-start(), calls=%async_computation.1 | async-start | bytes 3538944 | tf_op jit(solution)/shard_map/reduce_scatter | solution.py:106
  6.5 7.2 %collective-permute-start = (bf16[192,128]{1,0:T(8,128)(2,1)}, bf16[192,128]{1,0:T(8,128)(2,1)S(1)}, u32[]{:S(2)}, u32[]{:S(2)}) collective-permute-start(bf16[192,128]{1,0:T(8,128)(2,1)} %param.10), channel_id=1, source_target_pairs={{0,8},{8,16},{16,24},{24,32},{32,40},{40,48},{48,56},{56,64},{64,7... | collective-permute-start | bytes 147464 | tf_op jit(solution)/shard_map/ppermute | solution.py:14
  10.6 9.2 %collective-permute-start.4 = (bf16[192,128]{1,0:T(8,128)(2,1)}, bf16[192,128]{1,0:T(8,128)(2,1)S(1)}, u32[]{:S(2)}, u32[]{:S(2)}) collective-permute-start(bf16[192,128]{1,0:T(8,128)(2,1)} %param.11), channel_id=1, source_target_pairs={{0,8},{8,16},{16,24},{24,32},{32,40},{40,48},{48,56},{56,64},{64,7... | collective-permute-start | bytes 147464 | tf_op jit(solution)/shard_map/ppermute | solution.py:14
  14.6 10.3 %collective-permute-start.1 = (bf16[384,128]{1,0:T(8,128)(2,1)S(1)}, bf16[384,128]{1,0:T(8,128)(2,1)S(1)}, u32[]{:S(2)}, u32[]{:S(2)}) collective-permute-start(bf16[384,128]{1,0:T(8,128)(2,1)S(1)} %pad_maximum_fusion.4), channel_id=1, source_target_pairs={{0,16},{8,24},{16,32},{24,40},{32,48},{40,56},{48,64},{56,72},{64,... | collective-permute-start | bytes 294920 | tf_op jit(solution)/shard_map/ppermute | solution.py:14
  20.6 35.6 %copy-start.1 = (bf16[192,128]{1,0:T(8,128)(2,1)S(1)}, bf16[192,128]{1,0:T(8,128)(2,1)}, u32[]{:S(2)}) copy-start(bf16[192,128]{1,0:T(8,128)(2,1)} %param.10) | copy-start | bytes 147460
  20.6 10.7 %collective-permute-start.5 = (bf16[384,128]{1,0:T(8,128)(2,1)S(1)}, bf16[384,128]{1,0:T(8,128)(2,1)S(1)}, u32[]{:S(2)}, u32[]{:S(2)}) collective-permute-start(bf16[384,128]{1,0:T(8,128)(2,1)S(1)} %pad_maximum_fusion.5), channel_id=1, source_target_pairs={{0,16},{8,24},{16,32},{24,40},{32,48},{40,56},{48,64},{56,72},{64,... | collective-permute-start | bytes 294920 | tf_op jit(solution)/shard_map/ppermute | solution.py:14
  25.7 12.7 %collective-permute-start.2 = (bf16[768,128]{1,0:T(8,128)(2,1)S(1)}, bf16[768,128]{1,0:T(8,128)(2,1)S(1)}, u32[]{:S(2)}, u32[]{:S(2)}) collective-permute-start(bf16[768,128]{1,0:T(8,128)(2,1)S(1)} %pad_maximum_fusion.2), channel_id=1, source_target_pairs={{0,32},{8,40},{16,48},{24,56},{32,64},{40,72},{48,80},{56,88},{64,... | collective-permute-start | bytes 589832 | tf_op jit(solution)/shard_map/ppermute | solution.py:14
  32.2 13.1 %collective-permute-start.6 = (bf16[768,128]{1,0:T(8,128)(2,1)S(1)}, bf16[768,128]{1,0:T(8,128)(2,1)S(1)}, u32[]{:S(2)}, u32[]{:S(2)}) collective-permute-start(bf16[768,128]{1,0:T(8,128)(2,1)S(1)} %pad_maximum_fusion.3), channel_id=1, source_target_pairs={{0,32},{8,40},{16,48},{24,56},{32,64},{40,72},{48,80},{56,88},{64,... | collective-permute-start | bytes 589832 | tf_op jit(solution)/shard_map/ppermute | solution.py:14
  39.2 16.9 %collective-permute-start.3 = (bf16[1536,128]{1,0:T(8,128)(2,1)S(1)}, bf16[1536,128]{1,0:T(8,128)(2,1)S(1)}, u32[]{:S(2)}, u32[]{:S(2)}) collective-permute-start(bf16[1536,128]{1,0:T(8,128)(2,1)S(1)} %pad_maximum_fusion), channel_id=1, source_target_pairs={{0,64},{8,72},{16,80},{24,88},{32,96},{40,104},{48,112},{56,120},{... | collective-permute-start | bytes 1179656 | tf_op jit(solution)/shard_map/ppermute | solution.py:14
  45.3 18.1 %collective-permute-start.7 = (bf16[1536,128]{1,0:T(8,128)(2,1)S(1)}, bf16[1536,128]{1,0:T(8,128)(2,1)S(1)}, u32[]{:S(2)}, u32[]{:S(2)}) collective-permute-start(bf16[1536,128]{1,0:T(8,128)(2,1)S(1)} %pad_maximum_fusion.1), channel_id=1, source_target_pairs={{0,64},{8,72},{16,80},{24,88},{32,96},{40,104},{48,112},{56,120},{... | collective-permute-start | bytes 1179656 | tf_op jit(solution)/shard_map/ppermute | solution.py:14
Sparse Core Ops, SparseCore 0:
  83.8 92.8 reduce-scatter.1
where the time goes:
time: 184 us
  waiting for transfers between devices  100 us (54%)
  starting transfers between devices  44.2 us (24%)
  between operations  13.7 us (7%)
  matrix products  8.44 us (5%)
  local copies, waits for them, and re-layouts  6.34 us (3%)
  loops' own time  5.41 us (3%)
  other arithmetic  5.25 us (3%)
    reduce_scatter x1, waiting for transfers between devices, per_device(): lax.psum_scatter(jnp.dot(context, output_weight, preferred_element_type=j...  93.1 us
    ppermute x8, starting transfers between devices, shifted(): return lax.ppermute(block, axis, route)  44.2 us
    ppermute x8, waiting for transfers between devices, shifted(): return lax.ppermute(block, axis, route)  7.14 us
    dot_general x1, matrix products, per_device(): jnp.dot(context, output_weight, preferred_element_type=jnp.float32)  6.85 us
    another operation x1, loops' own time, per_device(): final_state = lax.fori_loop(0, part_rows // block_rows, one_block, initial)  5.3 us
  transfers between devices with their start and end apart: 9, of which 2 were waited for; matrix products, arithmetic and copies ran while one was open for 3% of the time, Pallas kernels for 0%

commit v1 on v0

v1 whole, which is shorter than its diff:
```python
import functools
import math

import jax
import jax.numpy as jnp
from jax import lax
from jax.experimental import pallas as pl
from jax.experimental.pallas import tpu as pltpu
from jax.sharding import PartitionSpec as P

MESH = pl.DeviceIdType.MESH
F32 = jnp.float32
BF16 = jnp.bfloat16

T = 192
HD = 128
G = 4
L = G * T
BACK = 12
NC = 8
CW = 512
HALF = 4096
ROWS = 24
UNIT = 2 * ROWS
NEG = -1e30
SCALE = math.log2(math.e) / math.sqrt(HD)
LT = 256


def kernel(
    q_hbm, k_hbm, v_hbm, doc_ref, w_hbm, out_ref,
    kb, vb, qb, wb, start_ref, max_ref, sum_ref, acc, ctx, ctxx,
    own, psend, precv, ownx, psendx, precvx, sbuf, rbuf,
    lsem, wsem, ksend, krecv, vsend, vrecv, csem, psem, pxsem, ssem, rsem,
):
    s = lax.axis_index("seq")
    t = lax.axis_index("tp")
    x = lax.rem(s, 8)
    row = s - x
    yl = t // 2
    c = lax.rem(t, 2)
    other = lax.rem(s + 64, 128)
    edge = (yl == 0) | (yl == 3)

    def in_row(step):
        return row + lax.rem(x + step + 8, 8)

    right = (in_row(1), t)
    left = (in_row(-1), t)
    up = (lax.rem(s + 8, 128), t)
    peer = (other, t)
    twin = (s, t + 1 - 2 * c)
    yl_in = jnp.where(yl < 2, yl + 1, yl - 1)
    yl_out = jnp.where((yl == 0) | (yl == 2), 3, 0)
    inward = (s, 2 * yl_in + c)
    outward = (jnp.where(edge, other, s), 2 * yl_out + c)

    q_copies = [
        pltpu.make_async_copy(
            q_hbm.at[:, pl.ds(h * HD, HD)], qb.at[pl.ds(h * T, T), :], lsem.at[h]
        )
        for h in range(G)
    ]
    k_copy = pltpu.make_async_copy(k_hbm, kb.at[0], lsem.at[G])
    v_copy = pltpu.make_async_copy(v_hbm, vb.at[0], lsem.at[G + 1])
    w_copy = pltpu.make_async_copy(w_hbm, wb, wsem)
    k_copy.start()
    v_copy.start()
    for copy in q_copies:
        copy.start()
    w_copy.start()

    barrier = pltpu.get_barrier_semaphore()
    friends = [(in_row(m), t) for m in (1, 2, 3, -1, -2, -3)]
    friends += [up, (lax.rem(s + 120, 128), t), peer, twin, inward, outward]
    for friend in friends:
        pl.semaphore_signal(barrier, inc=1, device_id=friend, device_id_type=MESH)
    pl.semaphore_wait(barrier, len(friends))

    def kv_copy(buf, send, recv, src, dst, sem, device):
        return pltpu.make_async_remote_copy(
            src_ref=buf.at[src], dst_ref=buf.at[dst],
            send_sem=send.at[sem], recv_sem=recv.at[dst],
            device_id=device, device_id_type=MESH,
        )

    def forward(d, buf, send, recv):
        mk = functools.partial(kv_copy, buf, send, recv)
        if d <= 3:
            @pl.when(x < 7)
            def _():
                mk(d, d + 1, d + 1, right).start()
        if 8 <= d <= 11:
            @pl.when(x == 7)
            def _():
                mk(d, d - 7, d - 7, right).start()
        if d <= 4:
            mk(d, d + 8, d + 8, up).start()
        if 6 <= d <= 8:
            @pl.when((x >= 1) & (x <= d - 1))
            def _():
                mk(d, d - 1, d - 1, left).start()
        if d == 0:
            for e in (7, 6, 5):
                @pl.when(x + e <= 7)
                def _(e=e):
                    mk(0, e, e + 8, (s + e, t)).start()

    def arrive(d):
        kv_copy(kb, ksend, krecv, d, d, d, left).wait_recv()
        forward(d, kb, ksend, krecv)
        kv_copy(vb, vsend, vrecv, d, d, d, left).wait_recv()
        forward(d, vb, vsend, vrecv)

    k_copy.wait()
    forward(0, kb, ksend, krecv)
    v_copy.wait()
    forward(0, vb, vsend, vrecv)

    first = (3 * s) // 2
    odd = lax.rem(s, 2)

    def column(r):
        vals = doc_ref[pl.ds(r, 1), :].astype(F32)
        return jnp.transpose(jnp.broadcast_to(vals, (HD, HD)))

    two = jnp.concatenate([column(first), column(first + 1)], axis=0)
    qdoc = jnp.where(odd == 0, two[:T], two[HD // 2:HD // 2 + T])
    span = 21
    low = jnp.clip(first - 18, 0, T - span)

    def count(n, total):
        vals = doc_ref[pl.ds(low + n, 1), :].astype(F32)
        return total + jnp.where(vals < qdoc, 1.0, 0.0)

    counted = lax.fori_loop(0, span, count, jnp.zeros((T, HD), F32))
    counted = jnp.transpose(jnp.concatenate([counted] * G, axis=0))
    begin = jnp.sum(counted, axis=0, keepdims=True).astype(jnp.int32)
    start_ref[...] = begin + (low * HD - s * T)

    for copy in q_copies:
        copy.wait()

    max_ref[...] = jnp.full((1, L), NEG, F32)
    sum_ref[...] = jnp.zeros((1, L), F32)
    acc[...] = jnp.zeros((HD, L), F32)

    def attend(d, diagonal=False):
        keys, values = kb[d], vb[d]
        for n in range(L // LT):
            cols = pl.ds(n * LT, LT)
            scores = lax.dot_general(
                keys, qb[cols, :], (((1,), (1,)), ((), ())), preferred_element_type=F32
            )
            pos = lax.broadcasted_iota(jnp.int32, (T, LT), 0)
            allowed = pos >= start_ref[:, cols] + d * T
            if diagonal:
                lane = n * LT + lax.broadcasted_iota(jnp.int32, (1, LT), 1)
                query = lane
                for h in range(1, G):
                    query = jnp.where(lane >= h * T, lane - h * T, query)
                allowed = allowed & (pos <= query)
            scores = jnp.where(allowed, scores * SCALE, NEG)
            old = max_ref[:, cols]
            new = jnp.maximum(old, jnp.max(scores, axis=0, keepdims=True))
            expo = jnp.exp2(scores - new)
            alpha = jnp.exp2(old - new)
            max_ref[:, cols] = new
            sum_ref[:, cols] = sum_ref[:, cols] * alpha + jnp.sum(expo, axis=0, keepdims=True)
            added = lax.dot_general(
                values, expo.astype(BF16), (((0,), (0,)), ((), ())), preferred_element_type=F32
            )
            acc[:, cols] = acc[:, cols] * alpha + added

    attend(0, True)

    def attend_all(slots):
        @pl.loop(0, len(slots))
        def _(n):
            slot = slots[-1]
            for m in range(len(slots) - 1):
                slot = jnp.where(n == m, slots[m], slot)
            attend(slot)

    for slots in ((8, 1), (7, 2, 9), (6, 3, 10), (5, 4, 11), (12,)):
        for d in slots:
            arrive(d)
        attend_all(slots)

    done = jnp.transpose(acc[...] / sum_ref[...])
    for h in range(G):
        ctx[:, h * HD:(h + 1) * HD] = done[h * T:(h + 1) * T].astype(BF16)

    swap = pltpu.make_async_remote_copy(
        src_ref=ctx.at[pl.ds(pl.multiple_of(UNIT * yl_out, 16), UNIT), :], dst_ref=ctxx,
        send_sem=csem.at[0], recv_sem=csem.at[1], device_id=peer, device_id_type=MESH,
    )

    @pl.when(edge)
    def _():
        swap.start()

    w_copy.wait()

    def partner_copy(j):
        return pltpu.make_async_remote_copy(
            src_ref=psend.at[j], dst_ref=precv.at[j],
            send_sem=psem.at[0, j], recv_sem=psem.at[1, j],
            device_id=twin, device_id_type=MESH,
        )

    def partner_copy_x(j):
        return pltpu.make_async_remote_copy(
            src_ref=psendx.at[j], dst_ref=precvx.at[j],
            send_sem=pxsem.at[0, j], recv_sem=pxsem.at[1, j],
            device_id=twin, device_id_type=MESH,
        )

    def send(kind, j, slot, device):
        return pltpu.make_async_remote_copy(
            src_ref=sbuf.at[kind, j], dst_ref=rbuf.at[slot, j],
            send_sem=ssem.at[kind, j], recv_sem=rsem.at[slot, j],
            device_id=device, device_id_type=MESH,
        )

    first_slot = jnp.where(edge, 0, 2)
    second_slot = jnp.where(edge, 1, 3)
    out_slot = jnp.where(edge, 1, 0)
    far = lax.rem(yl + 2, 4)

    def products(rows, j):
        wide = [
            jnp.dot(
                rows, wb[:, pl.ds(pl.multiple_of(base + j * CW, CW), CW)],
                preferred_element_type=F32,
            )
            for base in (0, HALF)
        ]
        pieces = []
        for d in range(rows.shape[0] // UNIT):
            cores = [
                jnp.concatenate(
                    [a[d * UNIT + k * ROWS:d * UNIT + (k + 1) * ROWS] for a in wide], axis=0
                )
                for k in range(2)
            ]
            pieces.append(
                (jnp.where(c == 0, cores[0], cores[1]), jnp.where(c == 0, cores[1], cores[0]))
            )
        return pieces

    def project(j):
        for d, (mine, theirs) in enumerate(products(ctx[...], j)):
            own[d, j] = mine
            psend[j, d] = theirs.astype(BF16)
        partner_copy(j).start()

    def combine(j):
        partner_copy(j).wait_recv()
        for d in range(4):
            own[d, j] = own[d, j] + precv[j, d].astype(F32)
        sbuf[0, j] = own[far, j].astype(BF16)
        send(0, j, first_slot, inward).start()

    project(0)

    @pl.loop(1, NC)
    def _(j):
        project(j)
        combine(j - 1)

    combine(NC - 1)

    @pl.when(edge)
    def _():
        @pl.loop(0, NC)
        def _(j):
            sbuf[1, j] = own[yl_in, j].astype(BF16)
            send(1, j, second_slot, inward).start()

        swap.wait_recv()

        def project_x(j):
            ((mine, theirs),) = products(ctxx[...], j)
            ownx[j] = mine
            psendx[j] = theirs.astype(BF16)
            partner_copy_x(j).start()

        def combine_x(j):
            partner_copy_x(j).wait_recv()
            sbuf[2, j] = (ownx[j] + precvx[j].astype(F32)).astype(BF16)
            send(2, j, out_slot, outward).start()

        project_x(0)

        @pl.loop(1, NC)
        def _(j):
            project_x(j)
            combine_x(j - 1)

        combine_x(NC - 1)

    @pl.when(jnp.logical_not(edge))
    def _():
        @pl.loop(0, NC)
        def _(j):
            send(0, j, 2, inward).wait_recv()
            sbuf[2, j] = (own[yl_out, j] + rbuf[2, j].astype(F32)).astype(BF16)
            send(2, j, out_slot, outward).start()
            send(0, j, 0, inward).wait_recv()
            sbuf[1, j] = (own[yl_in, j] + rbuf[0, j].astype(F32)).astype(BF16)
            send(1, j, second_slot, inward).start()

    last_a = jnp.where(edge, 0, 1)
    last_b = jnp.where(edge, 1, 3)

    @pl.loop(0, NC)
    def _(j):
        send(0, j, last_a, inward).wait_recv()
        send(0, j, last_b, inward).wait_recv()
        total = own[yl, j] + rbuf[last_a, j].astype(F32) + rbuf[last_b, j].astype(F32)
        total = total.astype(BF16)
        out_ref[:, pl.ds(pl.multiple_of(j * CW, CW), CW)] = total[:ROWS]
        out_ref[:, pl.ds(pl.multiple_of(HALF + j * CW, CW), CW)] = total[ROWS:]

    for buf, snd, rcv in ((kb, ksend, krecv), (vb, vsend, vrecv)):
        for d in (1, 2, 3, 4, 8, 9, 10, 11, 12):
            kv_copy(buf, snd, rcv, 0, d, d, left).wait_send()
        for d in (5, 6, 7):
            @pl.when((x >= 1) & (x <= d))
            def _(d=d):
                kv_copy(buf, snd, rcv, 0, d, d, left).wait_send()

            @pl.when(x + d <= 7)
            def _(d=d):
                kv_copy(buf, snd, rcv, 0, d, d + 8, left).wait_send()

    @pl.loop(0, NC)
    def _(j):
        partner_copy(j).wait_send()
        send(0, j, first_slot, inward).wait_send()
        send(1, j, second_slot, inward).wait_send()
        send(2, j, out_slot, outward).wait_send()

    @pl.when(edge)
    def _():
        swap.wait_send()

        @pl.loop(0, NC)
        def _(j):
            partner_copy_x(j).wait_send()


def per_device(query_rows, key_rows, value_rows, document_ids, output_weight):
    any_space = pl.BlockSpec(memory_space=pl.ANY)
    vmem = pl.BlockSpec(memory_space=pltpu.VMEM)
    dma = pltpu.SemaphoreType.DMA
    return pl.pallas_call(
        kernel,
        out_shape=jax.ShapeDtypeStruct((ROWS, 2 * HALF), BF16),
        in_specs=[any_space, any_space, any_space, vmem, any_space],
        out_specs=vmem,
        scratch_shapes=[
            pltpu.VMEM((BACK + 1, T, HD), BF16),
            pltpu.VMEM((BACK + 1, T, HD), BF16),
            pltpu.VMEM((L, HD), BF16),
            pltpu.VMEM((G * HD, 2 * HALF), BF16),
            pltpu.VMEM((1, L), jnp.int32),
            pltpu.VMEM((1, L), F32),
            pltpu.VMEM((1, L), F32),
            pltpu.VMEM((HD, L), F32),
            pltpu.VMEM((T, G * HD), BF16),
            pltpu.VMEM((UNIT, G * HD), BF16),
            pltpu.VMEM((4, NC, UNIT, CW), F32),
            pltpu.VMEM((NC, 4, UNIT, CW), BF16),
            pltpu.VMEM((NC, 4, UNIT, CW), BF16),
            pltpu.VMEM((NC, UNIT, CW), F32),
            pltpu.VMEM((NC, UNIT, CW), BF16),
            pltpu.VMEM((NC, UNIT, CW), BF16),
            pltpu.VMEM((3, NC, UNIT, CW), BF16),
            pltpu.VMEM((4, NC, UNIT, CW), BF16),
            dma((G + 2,)),
            dma,
            dma((16,)),
            dma((BACK + 1,)),
            dma((16,)),
            dma((BACK + 1,)),
            dma((2,)),
            dma((2, NC)),
            dma((2, NC)),
            dma((3, NC)),
            dma((4, NC)),
        ],
        compiler_params=pltpu.CompilerParams(
            collective_id=0, has_side_effects=True, vmem_limit_bytes=56 * 1024 * 1024
        ),
        name="attend_project",
    )(query_rows, key_rows, value_rows, document_ids.reshape(T, HD), output_weight)


def solution(mesh):
    in_specs = (P("seq", "tp"), P("seq", "tp"), P("seq", "tp"), P(), P("tp", None))
    out_specs = P(("seq", "tp"), None)
    return jax.shard_map(
        per_device, mesh=mesh, in_specs=in_specs, out_specs=out_specs, check_vma=False
    )
```

time: 184 us -> 81.8 us (0.44)
  waiting for transfers between devices: 100 us -> 0 us
  Pallas kernels: 0 us -> 79.9 us
  starting transfers between devices: 44.2 us -> 0 us
  between operations: 13.7 us -> 0.01 us
  matrix products: 8.44 us -> 0 us
  loops' own time: 5.41 us -> 0 us
  other arithmetic: 5.25 us -> 0 us
  local copies, waits for them, and re-layouts: 6.34 us -> 1.77 us
    reduce_scatter x1 -> x0, waiting for transfers between devices: 93.1 us -> none  [per_device(): lax.psum_scatter(jnp.dot(context, output_weight, preferred_element_type=j...]
    pallas_call x0 -> x1, Pallas kernels: none -> 79.9 us  [per_device(): pl.pallas_call(kernel, out_shape=jax.ShapeDtypeStruct((ROWS, 2 * HALF), B...]
    ppermute x8 -> x0, starting transfers between devices: 44.2 us -> none  [shifted(): return lax.ppermute(block, axis, route)]
    dot_general x3 -> x0, matrix products: 8.44 us -> none  [the longest x1 6.85 us: per_device(): jnp.dot(context, output_weight, preferred_element_type=jnp.float32)]
    ppermute x8 -> x0, waiting for transfers between devices: 7.14 us -> none  [shifted(): return lax.ppermute(block, axis, route)]
    another operation x5 -> x0, loops' own time: 5.41 us -> none  [the longest x1 5.3 us: per_device(): final_state = lax.fori_loop(0, part_rows // block_rows, one_block, initial)]
    concatenate x6 -> x0, other arithmetic: 4.1 us -> none  [the longest x3 2.45 us: per_device(): collected_keys = jnp.concatenate([earlier_keys, collected_keys], axis=0)]
    dynamic_slice x6 -> x0, local copies, waits for them, and re-layouts: 2.61 us -> none  [the longest x4 2.45 us: attend_block(): probe_doc = lax.dynamic_slice_in_dim(document_ids, probe, 1, 0)[0]]
  transfers between devices with their start and end apart: 9 -> 0, of which waited for: 2 -> 0; matrix products, arithmetic and copies ran while one was open for 3% -> 0% of each run, Pallas kernels for 0% -> 0%
where the time goes in v1:
time: 81.8 us; the launch traced here: 81.6 us
  Pallas kernels  79.9 us (98%)
  local copies, waits for them, and re-layouts  1.77 us (2%)
    pallas_call x1, Pallas kernels, per_device(): pl.pallas_call(kernel, out_shape=jax.ShapeDtypeStruct((ROWS, 2 * HALF), B...  79.9 us
    unnamed x1, local copies, waits for them, and re-layouts  1.77 us

profile of v1, /device:TPU:1, one launch (start us, length us, event | category | flops | bytes accessed | tf_op | source)
XLA Modules:
  0.0 81.6 jit_solution(8001214805098517255)
XLA Ops:
  0.0 79.9 %attend_project.1 = bf16[24,8192]{1,0:T(8,128)(2,1)} custom-call(bf16[192,512]{1,0:T(8,128)(2,1)} %q_hbm.1, bf16[192,128]{1,0:T(8,128)(2,1)} %k_hbm.1, bf16[192,128]{1,0:T(8,128)(2,1)} %v_hbm.1, s32[192,128]{1,0:T(8,128)} %bitcast.1, bf16[512,8192]{1,0:T(8,128)(2,1)} %w_hbm.1), custom_call_target="tpu_custom_call" | custom-call | tf_op jit(solution)/shard_map/attend_project/pallas_call | solution.py:358
  79.9 1.8 %copy.7 = bf16[24,8192]{1,0:T(8,128)(2,1)} copy(bf16[24,8192]{1,0:T(8,128)(2,1)} %attend_project.1) | data formatting | bytes 786432

commit v2 on v1

--- a/solution.py
+++ b/solution.py
@@ -23,15 +23,42 @@
 ROWS = 24
 UNIT = 2 * ROWS
 NEG = -1e30
+PARTS = 2
+PIECE = T
+SLOTS = 17
+TAIL = (9, 10, 11, 12)
+ORDER = [(8, 1, 7, 2, 6, 3, 5, 4) + TAIL]
+ORDER += [(1, 8, 2, 7, 3, 6, 4, 5) + TAIL] * 6
+ORDER += [(1, 8, 2, 9, 3, 10, 4, 11, 7, 6, 5, 12)]
+ORDER_Z0 = [
+    (8, 1, 7, 2, 6, 9, 3, 5, 10, 4, 11, 12),
+    (1, 8, 7, 9, 2, 6, 10, 3, 5, 4, 11, 12),
+    (1, 2, 8, 9, 7, 10, 6, 3, 5, 11, 4, 12),
+    (1, 2, 3, 8, 9, 7, 10, 6, 11, 5, 4, 12),
+    (1, 2, 3, 4, 8, 9, 7, 10, 6, 11, 5, 12),
+    (1, 2, 3, 4, 5, 8, 9, 7, 10, 6, 11, 12),
+    (1, 2, 3, 4, 6, 5, 8, 9, 7, 10, 11, 12),
+    (1, 2, 3, 4, 7, 6, 5, 8, 16, 9, 10, 11, 12),
+]
 SCALE = math.log2(math.e) / math.sqrt(HD)
-LT = 256
+LT = 384
+WORD = 6
+WORDS = 3
+
+
+def packed(order):
+    order = tuple(order) + (0,) * (WORD * WORDS - len(order))
+    return [
+        sum(d << (5 * n) for n, d in enumerate(order[w * WORD:(w + 1) * WORD]))
+        for w in range(WORDS)
+    ]
 
 
 def kernel(
     q_hbm, k_hbm, v_hbm, doc_ref, w_hbm, out_ref,
-    kb, vb, qb, wb, start_ref, max_ref, sum_ref, acc, ctx, ctxx,
+    kvb, qb, wb, start_ref, max_ref, sum_ref, acc, ctx, ctxx,
     own, psend, precv, ownx, psendx, precvx, sbuf, rbuf,
-    lsem, wsem, ksend, krecv, vsend, vrecv, csem, psem, pxsem, ssem, rsem,
+    lsem, wsem, kvsend, kvrecv, csem, psem, pxsem, ssem, rsem,
 ):
     s = lax.axis_index("seq")
     t = lax.axis_index("tp")
@@ -40,6 +67,11 @@
     yl = t // 2
     c = lax.rem(t, 2)
     other = lax.rem(s + 64, 128)
+    first_z = lax.rem(s, 64) < 8
+    last_z = lax.rem(s, 64) >= 56
+    across = (s >= 56) & (s < 64) & (x < 4)
+    far_source = s == 55
+    far_target = s == 71
     edge = (yl == 0) | (yl == 3)
 
     def in_row(step):
@@ -61,61 +93,85 @@
         )
         for h in range(G)
     ]
-    k_copy = pltpu.make_async_copy(k_hbm, kb.at[0], lsem.at[G])
-    v_copy = pltpu.make_async_copy(v_hbm, vb.at[0], lsem.at[G + 1])
+    kv_loads = [
+        pltpu.make_async_copy(
+            (k_hbm, v_hbm)[i], kvb.at[0, i], lsem.at[G + i],
+        )
+        for i in range(PARTS)
+    ]
     w_copy = pltpu.make_async_copy(w_hbm, wb, wsem)
-    k_copy.start()
-    v_copy.start()
+    for copy in kv_loads:
+        copy.start()
     for copy in q_copies:
         copy.start()
     w_copy.start()
 
     barrier = pltpu.get_barrier_semaphore()
-    friends = [(in_row(m), t) for m in (1, 2, 3, -1, -2, -3)]
-    friends += [up, (lax.rem(s + 120, 128), t), peer, twin, inward, outward]
+    friends = [(in_row(m), t) for m in (1, 2, -1, -2)]
+    friends += [(lax.rem(s + 120, 128), t), peer, twin, inward, outward]
     for friend in friends:
         pl.semaphore_signal(barrier, inc=1, device_id=friend, device_id_type=MESH)
-    pl.semaphore_wait(barrier, len(friends))
-
-    def kv_copy(buf, send, recv, src, dst, sem, device):
+    far_signal = (lax.rem(s + 112, 128), t)
+
+    @pl.when(far_target)
+    def _():
+        pl.semaphore_signal(barrier, inc=1, device_id=far_signal, device_id_type=MESH)
+
+    pl.semaphore_wait(barrier, len(friends) + jnp.where(far_source, 1, 0))
+
+    def kv_copy(src, dst, part, sem, device):
         return pltpu.make_async_remote_copy(
-            src_ref=buf.at[src], dst_ref=buf.at[dst],
-            send_sem=send.at[sem], recv_sem=recv.at[dst],
+            src_ref=kvb.at[src, part], dst_ref=kvb.at[dst, part],
+            send_sem=kvsend.at[sem, part], recv_sem=kvrecv.at[dst, part],
             device_id=device, device_id_type=MESH,
         )
 
-    def forward(d, buf, send, recv):
-        mk = functools.partial(kv_copy, buf, send, recv)
-        if d <= 3:
-            @pl.when(x < 7)
-            def _():
-                mk(d, d + 1, d + 1, right).start()
-        if 8 <= d <= 11:
-            @pl.when(x == 7)
-            def _():
-                mk(d, d - 7, d - 7, right).start()
-        if d <= 4:
-            mk(d, d + 8, d + 8, up).start()
-        if 6 <= d <= 8:
-            @pl.when((x >= 1) & (x <= d - 1))
-            def _():
-                mk(d, d - 1, d - 1, left).start()
-        if d == 0:
-            for e in (7, 6, 5):
-                @pl.when(x + e <= 7)
-                def _(e=e):
-                    mk(0, e, e + 8, (s + e, t)).start()
-
-    def arrive(d):
-        kv_copy(kb, ksend, krecv, d, d, d, left).wait_recv()
-        forward(d, kb, ksend, krecv)
-        kv_copy(vb, vsend, vrecv, d, d, d, left).wait_recv()
-        forward(d, vb, vsend, vrecv)
-
-    k_copy.wait()
-    forward(0, kb, ksend, krecv)
-    v_copy.wait()
-    forward(0, vb, vsend, vrecv)
+    def right_sem(to):
+        return jnp.where(to <= 4, to, to + 8)
+
+    def forward(d, part):
+        middle = (d >= 8) & (d <= 11)
+        passing = d >= 16
+
+        @pl.when(((x < 7) & ((d <= 3) | ((d == 4) & (x >= 4)) | (first_z & middle & (d <= x + 8)))) | ((x == 7) & (middle | passing)))
+        def _():
+            to = jnp.where(x < 7, d + 1, d - 7)
+            kv_copy(d, to, part, right_sem(to), right).start()
+
+        @pl.when(((d <= 4) & jnp.logical_not(last_z)) | (across & (d <= 4) & (d > jnp.maximum(x, 1 - x))))
+        def _():
+            kv_copy(d, d + 8, part, d + 8, up).start()
+
+        @pl.when((d >= 6) & (d <= 8) & (x >= 1) & (x <= d - 1))
+        def _():
+            kv_copy(d, d - 1, part, d - 1, left).start()
+
+    def direct(e):
+        @pl.when(x + e <= 7)
+        def _():
+            for part in range(PARTS):
+                kv_copy(0, e, part, e + 8, (s + e, t)).start()
+
+    for part, copy in enumerate(kv_loads):
+        copy.wait()
+
+        @pl.when(x < 7)
+        def _(part=part):
+            kv_copy(0, 1, part, 1, right).start()
+
+        @pl.when(s < 120)
+        def _(part=part):
+            kv_copy(0, 8, part, 8, up).start()
+
+        @pl.when(far_source)
+        def _(part=part):
+            kv_copy(0, 16, part, 16, (s + 16, t)).start()
+
+    direct(7)
+
+    @pl.when(first_z)
+    def _():
+        direct(6)
 
     first = (3 * s) // 2
     odd = lax.rem(s, 2)
@@ -146,7 +202,8 @@
     acc[...] = jnp.zeros((HD, L), F32)
 
     def attend(d, diagonal=False):
-        keys, values = kb[d], vb[d]
+        keys = kvb[d, 0]
+        values = kvb[d, 1]
         for n in range(L // LT):
             cols = pl.ds(n * LT, LT)
             scores = lax.dot_general(
@@ -174,18 +231,35 @@
 
     attend(0, True)
 
-    def attend_all(slots):
-        @pl.loop(0, len(slots))
-        def _(n):
-            slot = slots[-1]
-            for m in range(len(slots) - 1):
-                slot = jnp.where(n == m, slots[m], slot)
-            attend(slot)
-
-    for slots in ((8, 1), (7, 2, 9), (6, 3, 10), (5, 4, 11), (12,)):
-        for d in slots:
-            arrive(d)
-        attend_all(slots)
+    def order(index):
+        word = 0
+        for table, is_z0 in ((ORDER, False), (ORDER_Z0, True)):
+            for place in range(8):
+                here = (x == place) & (first_z if is_z0 else jnp.logical_not(first_z))
+                word = jnp.where(here, packed(table[place])[index], word)
+        return word
+
+    words = [order(index) for index in range(WORDS)]
+
+    @pl.loop(0, WORD * WORDS)
+    def _(n):
+        word = jnp.where(n < WORD, words[0], jnp.where(n < 2 * WORD, words[1], words[2]))
+        d = lax.shift_right_logical(word, 5 * lax.rem(n, WORD)) & 31
+        there = (d > 0) & (d <= s)
+
+        @pl.when(there)
+        def _():
+            for part in range(PARTS):
+                kv_copy(d, d, part, d, left).wait_recv()
+                forward(d, part)
+
+        @pl.when((n == 1) & jnp.logical_not(first_z))
+        def _():
+            direct(6)
+
+        @pl.when(there & (d <= BACK))
+        def _():
+            attend(d)
 
     done = jnp.transpose(acc[...] / sum_ref[...])
     for h in range(G):
@@ -323,17 +397,30 @@
         out_ref[:, pl.ds(pl.multiple_of(j * CW, CW), CW)] = total[:ROWS]
         out_ref[:, pl.ds(pl.multiple_of(HALF + j * CW, CW), CW)] = total[ROWS:]
 
-    for buf, snd, rcv in ((kb, ksend, krecv), (vb, vsend, vrecv)):
-        for d in (1, 2, 3, 4, 8, 9, 10, 11, 12):
-            kv_copy(buf, snd, rcv, 0, d, d, left).wait_send()
+    for part in range(PARTS):
+        def sent(sem, part=part):
+            kv_copy(0, 0, part, sem, left).wait_send()
+
+        for d in (1, 2, 3, 4):
+            pl.when(((x < 7) & (d - 1 <= s)) | ((x == 7) & (d + 7 <= s)))(
+                functools.partial(sent, d)
+            )
         for d in (5, 6, 7):
-            @pl.when((x >= 1) & (x <= d))
-            def _(d=d):
-                kv_copy(buf, snd, rcv, 0, d, d, left).wait_send()
-
-            @pl.when(x + d <= 7)
-            def _(d=d):
-                kv_copy(buf, snd, rcv, 0, d, d + 8, left).wait_send()
+            pl.when((x >= 1) & (x <= d) & (d + 1 <= s))(functools.partial(sent, d))
+            if d == 5:
+                pl.when((x >= 4) & (x <= 6) & (s >= 4))(functools.partial(sent, 13))
+            else:
+                pl.when(x + d <= 7)(functools.partial(sent, d + 8))
+        pl.when(s < 120)(functools.partial(sent, 8))
+        for d in (9, 10, 11, 12):
+            up_goes = jnp.logical_not(last_z) & (d - 8 <= s)
+            up_goes = up_goes | (across & (d - 8 > jnp.maximum(x, 1 - x)))
+            pl.when(up_goes)(functools.partial(sent, d))
+            late = first_z & (s >= 64)
+            if d >= 10:
+                late = late & (x < 7) & (x >= d - 9)
+            pl.when(late)(functools.partial(sent, d + 8))
+        pl.when(far_source)(functools.partial(sent, 16))
 
     @pl.loop(0, NC)
     def _(j):
@@ -357,12 +444,11 @@
     dma = pltpu.SemaphoreType.DMA
     return pl.pallas_call(
         kernel,
-        out_shape=jax.ShapeDtypeStruct((ROWS, 2 * HALF), BF16),
+        out_shape=pltpu.VMEM((ROWS, 2 * HALF), BF16),
         in_specs=[any_space, any_space, any_space, vmem, any_space],
         out_specs=vmem,
         scratch_shapes=[
-            pltpu.VMEM((BACK + 1, T, HD), BF16),
-            pltpu.VMEM((BACK + 1, T, HD), BF16),
+            pltpu.VMEM((SLOTS, PARTS, PIECE, HD), BF16),
             pltpu.VMEM((L, HD), BF16),
             pltpu.VMEM((G * HD, 2 * HALF), BF16),
             pltpu.VMEM((1, L), jnp.int32),
@@ -379,12 +465,10 @@
             pltpu.VMEM((NC, UNIT, CW), BF16),
             pltpu.VMEM((3, NC, UNIT, CW), BF16),
             pltpu.VMEM((4, NC, UNIT, CW), BF16),
-            dma((G + 2,)),
+            dma((G + PARTS,)),
             dma,
-            dma((16,)),
-            dma((BACK + 1,)),
-            dma((16,)),
-            dma((BACK + 1,)),
+            dma((21, PARTS)),
+            dma((SLOTS, PARTS)),
             dma((2,)),
             dma((2, NC)),
             dma((2, NC)),

time: 81.8 us -> 74.9 us (0.916)
  Pallas kernels: 79.9 us -> 74 us
  local copies, waits for them, and re-layouts: 1.77 us -> 0.75 us
    pallas_call x1, Pallas kernels: 79.9 us -> 74 us  [per_device(): pl.pallas_call(kernel, out_shape=pltpu.VMEM((ROWS, 2 * HALF), BF16), in_s...]
    unnamed x1, local copies, waits for them, and re-layouts: 1.77 us -> 0.75 us
where the time goes in v2:
time: 74.9 us; the launch traced here: 74.8 us
  Pallas kernels  74 us (99%)
  local copies, waits for them, and re-layouts  0.75 us (1%)
    pallas_call x1, Pallas kernels, per_device(): pl.pallas_call(kernel, out_shape=pltpu.VMEM((ROWS, 2 * HALF), BF16), in_s...  74 us

profile of v2, /device:TPU:1, one launch (start us, length us, event | category | flops | bytes accessed | tf_op | source)
XLA Modules:
  0.0 74.8 jit_solution(10161890475691654291)
XLA Ops:
  0.0 74.0 %attend_project.1 = bf16[24,8192]{1,0:T(8,128)(2,1)S(1)} custom-call(bf16[192,512]{1,0:T(8,128)(2,1)} %q_hbm.1, bf16[192,128]{1,0:T(8,128)(2,1)} %k_hbm.1, bf16[192,128]{1,0:T(8,128)(2,1)} %v_hbm.1, s32[192,128]{1,0:T(8,128)} %bitcast.1, bf16[512,8192]{1,0:T(8,128)(2,1)} %w_hbm.1), custom_call_target="tpu_custom_call" | custom-call | tf_op jit(solution)/shard_map/attend_project/pallas_call | solution.py:445
  74.0 0.7 %copy.7 = bf16[24,8192]{1,0:T(8,128)(2,1)} copy(bf16[24,8192]{1,0:T(8,128)(2,1)S(1)} %attend_project.1) | data formatting | bytes 786432

commit v3 on v2

--- a/solution.py
+++ b/solution.py
@@ -17,8 +17,8 @@
 G = 4
 L = G * T
 BACK = 12
-NC = 8
-CW = 512
+NC = 4
+CW = 1024
 HALF = 4096
 ROWS = 24
 UNIT = 2 * ROWS

time: 74.9 us -> 74.4 us (level)
  the two profiles are of different devices: /device:TPU:1 before, /device:TPU:97 now
where the time goes in v3:
time: 74.4 us; the launch traced here: 74.2 us
  Pallas kernels  73.4 us (99%)
  local copies, waits for them, and re-layouts  0.75 us (1%)
    pallas_call x1, Pallas kernels, per_device(): pl.pallas_call(kernel, out_shape=pltpu.VMEM((ROWS, 2 * HALF), BF16), in_s...  73.4 us

profile of v3, /device:TPU:97, one launch (start us, length us, event | category | flops | bytes accessed | tf_op | source)
XLA Modules:
  0.0 74.2 jit_solution(8867296549976175156)
XLA Ops:
  0.0 73.4 %attend_project.1 = bf16[24,8192]{1,0:T(8,128)(2,1)S(1)} custom-call(bf16[192,512]{1,0:T(8,128)(2,1)} %q_hbm.1, bf16[192,128]{1,0:T(8,128)(2,1)} %k_hbm.1, bf16[192,128]{1,0:T(8,128)(2,1)} %v_hbm.1, s32[192,128]{1,0:T(8,128)} %bitcast.1, bf16[512,8192]{1,0:T(8,128)(2,1)} %w_hbm.1), custom_call_target="tpu_custom_call" | custom-call | tf_op jit(solution)/shard_map/attend_project/pallas_call | solution.py:445
  73.4 0.7 %copy.7 = bf16[24,8192]{1,0:T(8,128)(2,1)} copy(bf16[24,8192]{1,0:T(8,128)(2,1)S(1)} %attend_project.1) | data formatting | bytes 786432
